TPU v7x, 256 devices: a whole 4x4x8 slice. The times are simulated.
256 devices in a mesh: dp: 32 (over z, x_hi, core), tensor: 8 (over y, x_lo).
Axes of the slice: x: 4 (x_hi: 2, x_lo: 2; x = x_hi * 2 + x_lo), y: 4, z: 8, core: 2. Of those that a mesh axis runs over, the one named last changes fastest.
Arguments:
- hidden_in: bfloat16 [12288, 4096], P('dp'), may hold values from -6 to 6
- upstream: bfloat16 [12288, 4096], P('dp'), may hold values from -6 to 6
- merged_input_weight: bfloat16 [4096, 6144], P('dp', 'tensor'), may hold values from -0.09375 to 0.09375
- output_matrix: bfloat16 [4096, 4096], P('dp', 'tensor'), may hold values from -0.09375 to 0.09375
- norm_gain: float32 [4096], replicated, may hold values from 0.5 to 1.5
- query_gain: float32 [128], replicated, may hold values from 0.5 to 1.5
- key_gain: float32 [128], replicated, may hold values from 0.5 to 1.5
Outputs:
- hidden_grad: bfloat16 [12288, 4096], P('dp')
- input_grad: float32 [4096, 6144], P('dp', 'tensor')
- output_grad: float32 [4096, 4096], P('dp', 'tensor')
- gain_grad: float32 [4096], replicated
- query_grad: float32 [128], replicated
- key_grad: float32 [128], replicated
All inputs are finite; a program needn't handle non-finite values.
Results may differ from a plain program's by a relative error of at most 0.015.
Values may be sent and summed in bfloat16 or wider, within the bound.
No kernel may reach another device: no remote copies, remote signals or barrier semaphores. Data moves between devices by JAX's collectives and lax.ppermute only.
A program may use at most 128 MiB of HBM per device.

v0:
```python
from functools import partial
import functools
import math
import jax
import jax.numpy as jnp
from jax import lax
from jax.sharding import Mesh
from jax.sharding import PartitionSpec as P

QUERY_HEADS = 32
KEY_VALUE_HEADS = 8
HEAD_SIZE = 128
TENSOR = ("tensor_0", "tensor_1")
DP = ("dp_0", "dp_1", "dp_2")
DP_TENSOR = ("dp_0", "dp_1", "dp_2", "tensor_0", "tensor_1")
EPSILON = 1e-06
ROPE_BASE = 1000000.0


def sent_to_all(x, axis):
    peers = lax.axis_size(axis)
    return lax.all_to_all(jnp.broadcast_to(x[None], (peers, *x.shape)), axis, 0, 0, tiled=True)


def joined_along(tiles, dim):
    lengths = list(tiles.shape[1:])
    lengths[dim] *= tiles.shape[0]
    return jnp.moveaxis(tiles, 0, dim).reshape(lengths)


def gathered_by_axis(x, axes, dim):
    far, near = axes
    tiles = sent_to_all(sent_to_all(x, far), near)
    return joined_along(tiles.swapaxes(0, 1).reshape(-1, *x.shape), dim)


def collect(x, axis, dim):
    tiles = sent_to_all(x, axis)
    return joined_along(tiles, dim)


def by_axis(x, axes):
    return functools.reduce(lax.psum, axes, x)


def norm_rows(states, scaling):
    inverse = lax.rsqrt(jnp.mean(states * states, axis=-1, keepdims=True) + EPSILON)
    return states * inverse * scaling


def rope_tables(length, columns):
    half_width = columns // 2
    exponent = jnp.arange(half_width, dtype=jnp.float32) * (2.0 / columns)
    frequency = jnp.exp(-exponent * math.log(ROPE_BASE))
    places = jnp.arange(length, dtype=jnp.float32)
    angles = places[:, None] * frequency[None, :]
    return (jnp.cos(angles), jnp.sin(angles))


def head_post(projected_rows, scaling, cosine, sine):
    inverse = lax.rsqrt(jnp.mean(projected_rows * projected_rows, axis=-1, keepdims=True) + EPSILON)
    normed = projected_rows * inverse * scaling
    half_width = projected_rows.shape[-1] // 2
    layout = (projected_rows.shape[0],) + (1,) * (projected_rows.ndim - 2) + (half_width,)
    cosine_part = cosine.reshape(layout)
    sine_part = sine.reshape(layout)
    leading = normed[..., :half_width]
    trailing = normed[..., half_width:]
    return jnp.concatenate(
        [
            leading * cosine_part - trailing * sine_part,
            trailing * cosine_part + leading * sine_part,
        ],
        axis=-1,
    )


def attend_forward(queries, keys, value_rows, score_scale):
    length = queries.shape[0]
    scores = (
        jnp.einsum("tkgh,skh->kgts", queries, keys, preferred_element_type=jnp.float32)
        * score_scale
    )
    causal = lax.broadcasted_iota(jnp.int32, (length, length), 0) >= lax.broadcasted_iota(
        jnp.int32, (length, length), 1
    )
    raised = jnp.where(causal, jnp.exp(scores), 0.0)
    softmax = raised / jnp.sum(raised, axis=-1, keepdims=True)
    softmax_low = softmax.astype(jnp.bfloat16)
    context = jnp.einsum(
        "kgts,skh->tkgh", softmax_low, value_rows, preferred_element_type=jnp.float32
    )
    return (softmax, softmax_low, context)


def attend_backward(queries, keys, value_rows, softmax, softmax_low, context_gradient, score_scale):
    grad_probs = jnp.einsum(
        "tkgh,skh->kgts", context_gradient, value_rows, preferred_element_type=jnp.float32
    )
    centre = jnp.sum(softmax * grad_probs, axis=-1, keepdims=True)
    grad_scores = (softmax * (grad_probs - centre) * score_scale).astype(jnp.bfloat16)
    grad_values = jnp.einsum(
        "kgts,tkgh->skh", softmax_low, context_gradient, preferred_element_type=jnp.float32
    )
    grad_queries = jnp.einsum(
        "kgts,skh->tkgh", grad_scores, keys, preferred_element_type=jnp.float32
    )
    grad_keys = jnp.einsum(
        "kgts,tkgh->skh", grad_scores, queries, preferred_element_type=jnp.float32
    )
    return (grad_queries, grad_keys, grad_values)


def local(hidden_in, upstream, merged_input_weight, output_matrix, norm_gain, query_gain, key_gain):
    shard_ranks = lax.axis_size(TENSOR)
    groups = lax.axis_size(DP)
    query_heads = QUERY_HEADS // shard_ranks
    key_head_rows = KEY_VALUE_HEADS // shard_ranks
    group_width = QUERY_HEADS // KEY_VALUE_HEADS
    query_columns = query_heads * HEAD_SIZE
    key_columns = key_head_rows * HEAD_SIZE
    score_scale = 1.0 / math.sqrt(HEAD_SIZE)
    length = hidden_in.shape[0]
    share = length // shard_ranks
    share_start = lax.axis_index(TENSOR) * share
    grad_scale = 1.0 / math.sqrt(groups * length)
    local_norm, norm_back = jax.vjp(norm_rows, hidden_in.astype(jnp.float32), norm_gain)
    normed = local_norm.astype(jnp.bfloat16)
    full_weight = lax.all_gather(merged_input_weight, DP, axis=0, tiled=True)
    projected_rows = jnp.dot(normed, full_weight, preferred_element_type=jnp.float32)
    unnormed_query = projected_rows[:, :query_columns].reshape(
        length, key_head_rows, group_width, HEAD_SIZE
    )
    unnormed_key = projected_rows[:, query_columns : query_columns + key_columns].reshape(
        length, key_head_rows, HEAD_SIZE
    )
    value_rows = (
        projected_rows[:, query_columns + key_columns :]
        .astype(jnp.bfloat16)
        .reshape(length, key_head_rows, HEAD_SIZE)
    )
    cosine, sine = rope_tables(length, HEAD_SIZE)
    post = partial(head_post, cosine=cosine, sine=sine)
    queries_full, query_back = jax.vjp(post, unnormed_query, query_gain)
    keys_full, key_back = jax.vjp(post, unnormed_key, key_gain)
    queries = queries_full.astype(jnp.bfloat16)
    keys = keys_full.astype(jnp.bfloat16)
    context_gradient = jnp.dot(
        upstream,
        gathered_by_axis(output_matrix, (("dp_0", "dp_1"), "dp_2"), 0),
        preferred_element_type=jnp.float32,
    )
    context_gradient = context_gradient.astype(jnp.bfloat16).reshape(
        length, key_head_rows, group_width, HEAD_SIZE
    )
    softmax, softmax_low, context = attend_forward(queries, keys, value_rows, score_scale)
    context_low = context.astype(jnp.bfloat16).reshape(length, query_columns)
    grad_queries, grad_keys, grad_values = attend_backward(
        queries, keys, value_rows, softmax, softmax_low, context_gradient, score_scale
    )
    grad_raw_query, query_part = query_back(grad_queries)
    grad_raw_key, key_part = key_back(grad_keys)
    grad_projected = jnp.concatenate(
        [
            grad_raw_query.reshape(length, query_columns),
            grad_raw_key.reshape(length, key_columns),
            grad_values.reshape(length, key_columns),
        ],
        axis=1,
    ).astype(jnp.bfloat16)
    own_hidden = lax.dynamic_slice_in_dim(hidden_in, share_start, share, 0).astype(jnp.float32)
    own_upstream = lax.dynamic_slice_in_dim(upstream, share_start, share, 0).astype(jnp.float32)
    rows = grad_projected
    grad_share = lax.psum_scatter(
        lax.dot_general(
            rows, full_weight, (((1,), (1,)), ((), ())), preferred_element_type=jnp.float32
        ).astype(jnp.bfloat16),
        TENSOR,
        scatter_dimension=0,
        tiled=True,
    ).astype(jnp.float32)
    share_norm, share_back = jax.vjp(norm_rows, own_hidden, norm_gain)
    grad_own, gain_part = share_back(grad_share)
    own_rows = (own_upstream + grad_own).astype(jnp.bfloat16)
    hidden_grad = collect(own_rows, TENSOR, 0)
    rows = upstream
    joined = lax.psum_scatter(
        jnp.concatenate(
            [
                lax.dot_general(
                    normed,
                    grad_projected,
                    (((0,), (0,)), ((), ())),
                    preferred_element_type=jnp.float32,
                )
                * grad_scale,
                lax.dot_general(
                    rows, context_low, (((0,), (0,)), ((), ())), preferred_element_type=jnp.float32
                )
                * grad_scale,
            ],
            axis=1,
        ).astype(jnp.bfloat16),
        DP,
        scatter_dimension=0,
        tiled=True,
    ).astype(jnp.float32)
    input_grad = joined[:, : merged_input_weight.shape[1]]
    output_grad = joined[:, merged_input_weight.shape[1] :]
    gain_sum, query_sum, key_sum = (
        by_axis(gain_part, DP_TENSOR),
        by_axis(query_part, DP_TENSOR),
        by_axis(key_part, DP_TENSOR),
    )
    return (
        hidden_grad,
        input_grad,
        output_grad,
        gain_sum * grad_scale,
        query_sum * grad_scale,
        key_sum * grad_scale,
    )


def solution(mesh):
    split = Mesh(
        mesh.devices.reshape(8, 2, 2, 4, 2), ("dp_0", "dp_1", "dp_2", "tensor_0", "tensor_1")
    )
    return jax.shard_map(
        local,
        mesh=split,
        in_specs=(P(DP, None), P(DP, None), P(DP, TENSOR), P(DP, TENSOR), P(), P(), P()),
        out_specs=(P(DP, None), P(DP, TENSOR), P(DP, TENSOR), P(), P(), P()),
        check_vma=False,
    )
```

profile of v0, /device:TPU:16, one launch (start us, length us, event | category | flops | bytes accessed | tf_op | source)
XLA Modules:
  0.0 413.0 jit_solution(11198640419863443358)
XLA Ops:
  7.9 2.4 broadcast_in_dim.22
  10.3 11.0 %all-to-all-start = ((bf16[16,128,512]{2,1,0:T(8,128)(2,1)}), bf16[16,128,512]{2,1,0:T(8,128)(2,1)S(1)}, u32[]{:S(2)}, u32[]{:S(2)}) async-start(bf16[16,128,512]{2,1,0:T(8,128)(2,1)} %broadcast_in_dim.22), calls=%async_computation | async-start | bytes 4194304 | tf_op jit(solution)/shard_map/all_to_all | solution.py:22
  22.1 2.6 fusion
  26.1 54.7 %all-to-all-done = bf16[16,128,512]{2,1,0:T(8,128)(2,1)S(1)} async-done(((bf16[16,128,512]{2,1,0:T(8,128)(2,1)}), bf16[16,128,512]{2,1,0:T(8,128)(2,1)S(1)}, u32[]{:S(2)}, u32[]{:S(2)}) %all-to-all-start) | async-done | bytes 2097184 | tf_op jit(solution)/shard_map/all_to_all | solution.py:22
  81.3 7.1 %all_to_all.15 = bf16[2,16,128,512]{3,2,1,0:T(8,128)(2,1)S(1)} all-to-all(bf16[2,16,128,512]{3,2,1,0:T(8,128)(2,1)S(1)} %broadcast_in_dim.23), channel_id=1, replica_groups=mesh['dp_0'=8,'dp_1'=2,'dp_2'=2,'tensor_0'=4,'tensor_1'=2] {'dp_2'}, dimensions={0} | all-to-all | bytes 8388608 | tf_op jit(solution)/shard_map/all_to_all | solution.py:22
  90.3 2.5 convolution_convert_fusion.2
  92.8 1.9 copy.126
  94.7 32.5 %all-gather.2.cloned.1.call-done = bf16[4096,768]{1,0:T(8,128)(2,1)} async-done(((bf16[128,768]{1,0:T(8,128)(2,1)}), bf16[4096,768]{1,0:T(8,128)(2,1)}) %all-gather.2.cloned.1.call-update) | async-done | bytes 6291472 | tf_op jit(solution)/shard_map/all_gather | solution.py:129
  127.2 5.4 %fusion.26 = f32[384,768]{1,0:T(8,128)S(1)} fusion(bf16[4096,768]{1,0:T(8,128)(2,1)} %all-gather.2.cloned.1.call-done, bf16[384,4096]{1,0:T(8,128)(2,1)S(1)} %copy-done, f32[4096]{0:T(1024)S(1)} %copy-done.10, f32[384]{0:T(512)} %add_rsqrt_fusion), kind=kOutput, calls=%fused_computation.40 | convolution fusion | flops 2422210560 | bytes 10634752 | tf_op jit(solution)/shard_map/dot_general | solution.py:130
  151.2 7.1 %convolution_convert_fusion = bf16[384,4096]{1,0:T(8,128)(2,1)} fusion(bf16[4096,768]{1,0:T(8,128)(2,1)} %all-gather.2.cloned.1.call-done, bf16[384,128]{0,1:T(8,128)(2,1)S(1)} %copy-done.29, bf16[384,128]{0,1:T(8,128)(2,1)S(1)} %copy.107, bf16[384,512]{0,1:T(8,128)(2,1)S(1)} %bitcast.135), kind=kOutput, calls=%fused_computation.8 | convolution fusion | flops 2419261440 | bytes 10027008 | tf_op jit(solution)/shard_map/dot_general | solution.py:175
  159.2 1.9 convolution_convert_fusion.1
  161.2 2.3 fusion.3
  163.6 3.9 multiply_convert_fusion
  167.5 9.6 %pad_maximum_fusion = bf16[4096,1280]{0,1:T(8,128)(2,1)} fusion(bf16[4096,512]{0,1:T(8,128)(2,1)S(1)} %fusion.3, bf16[4096,768]{0,1:T(8,128)(2,1)S(1)} %multiply_convert_fusion), kind=kLoop, calls=%fused_computation.1 | loop fusion | flops 20971520 | bytes 20971520 | tf_op jit(solution)/shard_map/concatenate | solution.py:188
  177.0 14.4 %copy.124 = bf16[4096,1280]{1,0:T(8,128)(2,1)} copy(bf16[4096,1280]{0,1:T(8,128)(2,1)} %pad_maximum_fusion) | data formatting | bytes 20971520
  191.7 36.7 %reduce-scatter.5.cloned.1.call-done = bf16[48,4096]{1,0:T(8,128)(2,1)} async-done(((bf16[384,4096]{1,0:T(8,128)(2,1)}), bf16[48,4096]{1,0:T(8,128)(2,1)}) %reduce-scatter.5.cloned.1.call-update) | async-done | bytes 393232 | tf_op jit(solution)/shard_map/reduce_scatter | solution.py:174
  231.2 2.0 broadcast_in_dim.27
  233.2 5.6 %all-to-all-start.2 = ((bf16[8,48,4096]{2,1,0:T(8,128)(2,1)}), bf16[8,48,4096]{2,1,0:T(8,128)(2,1)S(1)}, u32[]{:S(2)}, u32[]{:S(2)}) async-start(bf16[8,48,4096]{2,1,0:T(8,128)(2,1)} %broadcast_in_dim.27), calls=%async_computation.3 | async-start | bytes 6291456 | tf_op jit(solution)/shard_map/all_to_all | solution.py:22
  238.8 30.2 %all-reduce.4 = (f32[4096]{0:T(1024)S(1)}, f32[128]{0:T(128)S(1)}, f32[128]{0:T(128)S(1)}) all-reduce(f32[4096]{0:T(1024)S(1)} %get-tuple-element.36, f32[128]{0:T(128)S(1)} %get-tuple-element.38, f32[128]{0:T(128)S(1)} %get-tuple-element.40), channel_id=1, replica_groups=mesh['dp_0'=8,'dp_1'=2,'dp_2'=2,'tensor_0'=4,'tensor_1'=2] {'dp_0'}, use_global_device_ids=true, to_apply=%region_12.13 | all-reduce | flops 4352 | bytes 34816 | tf_op jit(solution)/shard_map/psum | solution.py:43
  269.0 11.1 %all-reduce.8 = (f32[4096]{0:T(1024)S(1)}, f32[128]{0:T(128)S(1)}, f32[128]{0:T(128)S(1)}) all-reduce(f32[4096]{0:T(1024)S(1)} %get-tuple-element.42, f32[128]{0:T(128)S(1)} %get-tuple-element.43, f32[128]{0:T(128)S(1)} %get-tuple-element.44), channel_id=1, replica_groups=mesh['dp_0'=8,'dp_1'=2,'dp_2'=2,'tensor_0'=4,'tensor_1'=2] {'dp_1'}, use_global_device_ids=true, to_apply=%region_13.14 | all-reduce | flops 4352 | bytes 34816 | tf_op jit(solution)/shard_map/psum | solution.py:43
  280.1 3.4 all-reduce.7
  283.5 15.4 %all-reduce.5 = (f32[4096]{0:T(1024)S(1)}, f32[128]{0:T(128)S(1)}, f32[128]{0:T(128)S(1)}) all-reduce(f32[4096]{0:T(1024)S(1)} %get-tuple-element.51, f32[128]{0:T(128)S(1)} %get-tuple-element.52, f32[128]{0:T(128)S(1)} %get-tuple-element.53), channel_id=1, replica_groups=mesh['dp_0'=8,'dp_1'=2,'dp_2'=2,'tensor_0'=4,'tensor_1'=2] {'tensor_0'}, use_global_device_ids=true, to_apply=%region_15.16 | all-reduce | flops 4352 | bytes 34816 | tf_op jit(solution)/shard_map/psum | solution.py:43
  299.0 8.0 %all-reduce.6 = (f32[4096]{0:T(1024)S(1)}, f32[128]{0:T(128)S(1)}, f32[128]{0:T(128)S(1)}) all-reduce(f32[4096]{0:T(1024)S(1)} %get-tuple-element.45, f32[128]{0:T(128)S(1)} %get-tuple-element.46, f32[128]{0:T(128)S(1)} %get-tuple-element.47), channel_id=1, replica_groups=mesh['dp_0'=8,'dp_1'=2,'dp_2'=2,'tensor_0'=4,'tensor_1'=2] {'tensor_1'}, use_global_device_ids=true, to_apply=%region_16.17 | all-reduce | flops 4352 | bytes 34816 | tf_op jit(solution)/shard_map/psum | solution.py:43
  308.1 89.4 %reduce-scatter.7.cloned.1.call-done = bf16[128,1280]{1,0:T(8,128)(2,1)} async-done(((bf16[4096,1280]{1,0:T(8,128)(2,1)}), bf16[128,1280]{1,0:T(8,128)(2,1)}) %reduce-scatter.7.cloned.1.call-update) | async-done | bytes 327696
  (114 shorter events, 37.5 us)
Async XLA Ops:
  7.2 120.1 %all-gather.2.cloned.1.call-start = ((), (), s32[]{:S(2)}) async-start(), calls=%async_computation.5 | async-start | bytes 6488064 | tf_op jit(solution)/shard_map/all_gather | solution.py:129
  10.3 70.4 %all-to-all-start = ((bf16[16,128,512]{2,1,0:T(8,128)(2,1)}), bf16[16,128,512]{2,1,0:T(8,128)(2,1)S(1)}, u32[]{:S(2)}, u32[]{:S(2)}) async-start(bf16[16,128,512]{2,1,0:T(8,128)(2,1)} %broadcast_in_dim.22), calls=%async_computation | async-start | bytes 4194304 | tf_op jit(solution)/shard_map/all_to_all | solution.py:22
  21.4 207.0 %reduce-scatter.5.cloned.1.call-start = ((), (), s32[]{:S(2)}) async-start(), calls=%async_computation.6 | async-start | bytes 3538944 | tf_op jit(solution)/shard_map/reduce_scatter | solution.py:174
  21.4 59.8 %copy-start.25 = (f32[64]{0:T(128)}, f32[64]{0:T(128)S(1)}, u32[]{:S(2)}) copy-start(f32[64]{0:T(128)S(1)} %multiply_exponential_fusion) | copy-start | bytes 772
  26.0 110.9 %copy-start.3 = (f32[384,64]{1,0:T(8,128)}, f32[384,64]{1,0:T(8,128)S(1)}, u32[]{:S(2)}) copy-start(f32[384,64]{1,0:T(8,128)S(1)} %get-tuple-element.66) | copy-start | bytes 294916
  90.3 37.0 %copy-start = (bf16[384,4096]{1,0:T(8,128)(2,1)S(1)}, bf16[384,4096]{1,0:T(8,128)(2,1)}, u32[]{:S(2)}) copy-start(bf16[384,4096]{1,0:T(8,128)(2,1)} %param.7) | copy-start | bytes 9437188
  90.3 37.0 %copy-start.10 = (f32[4096]{0:T(1024)S(1)}, f32[4096]{0:T(1024)}, u32[]{:S(2)}) copy-start(f32[4096]{0:T(1024)} %param.11) | copy-start | bytes 49156
  132.7 3.1 copy-start.26
  133.7 2.9 copy-start.21
  133.9 3.1 copy-start.17
  134.7 2.6 copy-start.11
  134.8 2.6 copy-start.15
  138.3 3.8 copy-start.19
  144.9 2.7 copy-start.27
  144.9 3.8 copy-start.16
  144.9 3.8 copy-start.24
  145.0 4.9 %copy-start.18 = (f32[384]{0:T(512)S(1)}, f32[384]{0:T(512)}, u32[]{:S(2)}) copy-start(f32[384]{0:T(512)} %copy-done.17) | copy-start | bytes 4612
  145.0 6.2 %copy-start.29 = (bf16[384,128]{0,1:T(8,128)(2,1)S(1)}, bf16[384,128]{0,1:T(8,128)(2,1)}, u32[]{:S(2)}) copy-start(bf16[384,128]{0,1:T(8,128)(2,1)} %fusion.20) | copy-start | bytes 294916
  147.6 3.5 copy-start.8
  158.3 239.1 %reduce-scatter.7.cloned.1.call-start = ((), (), s32[]{:S(2)}) async-start(), calls=%async_computation.7 | async-start | bytes 10813440
  161.2 2.4 copy-start.1
  161.2 2.4 copy-start.9
  161.2 2.4 copy-start.28
  233.2 74.8 %all-to-all-start.2 = ((bf16[8,48,4096]{2,1,0:T(8,128)(2,1)}), bf16[8,48,4096]{2,1,0:T(8,128)(2,1)S(1)}, u32[]{:S(2)}, u32[]{:S(2)}) async-start(bf16[8,48,4096]{2,1,0:T(8,128)(2,1)} %broadcast_in_dim.27), calls=%async_computation.3 | async-start | bytes 6291456 | tf_op jit(solution)/shard_map/all_to_all | solution.py:22
  (11 other events, 14.9 us)
Sparse Core Ops, SparseCore 0:
  10.7 116.4 all-gather.1
  158.5 69.8 reduce-scatter.4
  232.8 164.6 reduce-scatter.6
where the time goes:
time: 414 us; the launch traced here: 413 us
  waiting for transfers between devices  214 us (52%)
  blocking collectives  75.2 us (18%)
  local copies, waits for them, and re-layouts  36.3 us (9%)
  matrix products  28.4 us (7%)
  other arithmetic  28.1 us (7%)
  starting transfers between devices  16.7 us (4%)
  between operations  14.3 us (3%)
    unnamed x4, waiting for transfers between devices  90.1 us
    psum x5, blocking collectives, by_axis(): return functools.reduce(lax.psum, axes, x)  68.1 us
    all_to_all x2, waiting for transfers between devices, sent_to_all(): lax.all_to_all(jnp.broadcast_to(x[None], (peers, *x.shape)), axis, 0, 0,...  54.7 us
    reduce_scatter x1, waiting for transfers between devices, local(): lax.psum_scatter(lax.dot_general(rows, full_weight, (((1,), (1,)), ((), (...  36.7 us
    all_gather x1, waiting for transfers between devices, local(): full_weight = lax.all_gather(merged_input_weight, DP, axis=0, tiled=True)  32.5 us
    unnamed x66, local copies, waits for them, and re-layouts  24.6 us
    all_to_all x2, starting transfers between devices, sent_to_all(): lax.all_to_all(jnp.broadcast_to(x[None], (peers, *x.shape)), axis, 0, 0,...  16.6 us
    concatenate x1, other arithmetic, local(): jnp.concatenate([lax.dot_general(normed, grad_projected, (((0,), (0,)), (...  9.55 us
  transfers between devices with their start and end apart: 5, of which 4 were waited for; matrix products, arithmetic and copies ran while one was open for 12% of the time, Pallas kernels for 0%

commit v1 on v0

--- a/solution.py
+++ b/solution.py
@@ -126,7 +126,10 @@
     grad_scale = 1.0 / math.sqrt(groups * length)
     local_norm, norm_back = jax.vjp(norm_rows, hidden_in.astype(jnp.float32), norm_gain)
     normed = local_norm.astype(jnp.bfloat16)
-    full_weight = lax.all_gather(merged_input_weight, DP, axis=0, tiled=True)
+    n_dev = lax.axis_size(DP)
+    blocks = jnp.stack([merged_input_weight for _ in range(n_dev)])
+    blocks = lax.all_to_all(blocks, DP, split_axis=0, concat_axis=0)
+    full_weight = jnp.concatenate(blocks, axis=0)
     projected_rows = jnp.dot(normed, full_weight, preferred_element_type=jnp.float32)
     unnormed_query = projected_rows[:, :query_columns].reshape(
         length, key_head_rows, group_width, HEAD_SIZE

time: 414 us -> 517 us (1.25)
  blocking collectives: 75.2 us -> 140 us
  waiting for transfers between devices: 214 us -> 257 us
  starting transfers between devices: 16.7 us -> 10.8 us
    all_to_all x0 -> x1, waiting for transfers between devices: none -> 131 us  [local(): blocks = lax.all_to_all(blocks, DP, split_axis=0, concat_axis=0)]
    all_to_all x1 -> x2, blocking collectives: 7.1 us -> 71.6 us  [sent_to_all(): lax.all_to_all(jnp.broadcast_to(x[None], (peers, *x.shape)), axis, 0, 0,...]
    all_to_all x2 -> x1, waiting for transfers between devices: 54.7 us -> 0.01 us  [sent_to_all(): lax.all_to_all(jnp.broadcast_to(x[None], (peers, *x.shape)), axis, 0, 0,...]
    all_gather x1 -> x0, waiting for transfers between devices: 32.5 us -> none  [local(): full_weight = lax.all_gather(merged_input_weight, DP, axis=0, tiled=True)]
    all_to_all x2 -> x1, starting transfers between devices: 16.6 us -> 5.55 us  [sent_to_all(): lax.all_to_all(jnp.broadcast_to(x[None], (peers, *x.shape)), axis, 0, 0,...]
    unnamed x66 -> x68, local copies, waits for them, and re-layouts: 24.6 us -> 23.6 us
    unnamed x4 -> x3, waiting for transfers between devices: 90.1 us -> 89.4 us
  transfers between devices with their start and end apart: 5 -> 4, of which waited for: 4 -> 3; matrix products, arithmetic and copies ran while one was open for 12% -> 9% of each run, Pallas kernels for 0% -> 0%
where the time goes in v1:
time: 517 us; the launch traced here: 516 us
  waiting for transfers between devices  257 us (50%)
  blocking collectives  140 us (27%)
  local copies, waits for them, and re-layouts  39.8 us (8%)
  matrix products  28.4 us (5%)
  other arithmetic  26.1 us (5%)
  between operations  14.6 us (3%)
  starting transfers between devices  10.8 us (2%)
    all_to_all x1, waiting for transfers between devices, local(): blocks = lax.all_to_all(blocks, DP, split_axis=0, concat_axis=0)  131 us
    unnamed x3, waiting for transfers between devices  89.4 us
    all_to_all x2, blocking collectives, sent_to_all(): lax.all_to_all(jnp.broadcast_to(x[None], (peers, *x.shape)), axis, 0, 0,...  71.6 us
    psum x5, blocking collectives, by_axis(): return functools.reduce(lax.psum, axes, x)  68.1 us
    reduce_scatter x1, waiting for transfers between devices, local(): lax.psum_scatter(lax.dot_general(rows, full_weight, (((1,), (1,)), ((), (...  36 us
    unnamed x68, local copies, waits for them, and re-layouts  23.6 us
  transfers between devices with their start and end apart: 4, of which 3 were waited for; matrix products, arithmetic and copies ran while one was open for 9% of the time, Pallas kernels for 0%

profile of v1, /device:TPU:16, one launch (start us, length us, event | category | flops | bytes accessed | tf_op | source)
XLA Modules:
  0.0 516.1 jit_solution(3768609389358958970)
XLA Ops:
  8.3 63.4 %all_to_all.20 = bf16[16,128,512]{2,1,0:T(8,128)(2,1)S(1)} all-to-all(bf16[16,128,512]{2,1,0:T(8,128)(2,1)S(1)} %broadcast_in_dim.22), channel_id=1, replica_groups=mesh['dp_0'=8,'dp_1'=2,'dp_2'=2,'tensor_0'=4,'tensor_1'=2] {'dp_0','dp_1'}, dimensions={0} | all-to-all | bytes 4194304 | tf_op jit(solution)/shard_map/all_to_all | solution.py:22
  72.2 8.3 %all_to_all.21 = bf16[2,16,128,512]{3,2,1,0:T(8,128)(2,1)} all-to-all(bf16[2,16,128,512]{3,2,1,0:T(8,128)(2,1)S(1)} %broadcast_in_dim.23), channel_id=1, replica_groups=mesh['dp_0'=8,'dp_1'=2,'dp_2'=2,'tensor_0'=4,'tensor_1'=2] {'dp_2'}, dimensions={0} | all-to-all | bytes 8388608 | tf_op jit(solution)/shard_map/all_to_all | solution.py:22
  80.5 3.4 stack.2
  83.9 5.2 all-to-all-start
  91.9 2.8 copy.94
  95.1 2.5 convolution_convert_fusion.2
  97.7 1.9 copy.126
  99.6 131.2 %all-to-all-done = bf16[32,128,768]{2,1,0:T(8,128)(2,1)} async-done(((bf16[32,128,768]{2,1,0:T(8,128)(2,1)}), bf16[32,128,768]{2,1,0:T(8,128)(2,1)}, u32[]{:S(2)}, u32[]{:S(2)}) %all-to-all-start) | async-done | bytes 6291488 | tf_op jit(solution)/shard_map/all_to_all | solution.py:131
  230.8 5.4 %fusion.26 = f32[384,768]{1,0:T(8,128)S(1)} fusion(bf16[4096,768]{1,0:T(8,128)(2,1)} %bitcast, bf16[384,4096]{1,0:T(8,128)(2,1)S(1)} %copy-done, f32[4096]{0:T(1024)S(1)} %copy-done.11, f32[384]{0:T(512)} %add_rsqrt_fusion), kind=kOutput, calls=%fused_computation.40 | convolution fusion | flops 2422210560 | bytes 10634752 | tf_op jit(solution)/shard_map/dot_general | solution.py:133
  254.7 7.1 %convolution_convert_fusion = bf16[384,4096]{1,0:T(8,128)(2,1)} fusion(bf16[4096,768]{1,0:T(8,128)(2,1)} %bitcast, bf16[384,128]{0,1:T(8,128)(2,1)S(1)} %copy-done.30, bf16[384,128]{0,1:T(8,128)(2,1)S(1)} %copy.107, bf16[384,512]{0,1:T(8,128)(2,1)S(1)} %bitcast.136), kind=kOutput, calls=%fused_computation.8 | convolution fusion | flops 2419261440 | bytes 10027008 | tf_op jit(solution)/shard_map/dot_general | solution.py:178
  262.7 1.8 convolution_convert_fusion.1
  264.7 2.3 fusion.3
  267.1 3.9 multiply_convert_fusion
  271.0 9.5 %pad_maximum_fusion = bf16[4096,1280]{0,1:T(8,128)(2,1)} fusion(bf16[4096,512]{0,1:T(8,128)(2,1)S(1)} %fusion.3, bf16[4096,768]{0,1:T(8,128)(2,1)S(1)} %multiply_convert_fusion), kind=kLoop, calls=%fused_computation.1 | loop fusion | flops 20971520 | bytes 20971520 | tf_op jit(solution)/shard_map/concatenate | solution.py:191
  280.5 14.5 %copy.124 = bf16[4096,1280]{1,0:T(8,128)(2,1)} copy(bf16[4096,1280]{0,1:T(8,128)(2,1)} %pad_maximum_fusion) | data formatting | bytes 20971520
  295.2 36.0 %reduce-scatter.5.cloned.1.call-done = bf16[48,4096]{1,0:T(8,128)(2,1)} async-done(((bf16[384,4096]{1,0:T(8,128)(2,1)}), bf16[48,4096]{1,0:T(8,128)(2,1)}) %reduce-scatter.5.cloned.1.call-update) | async-done | bytes 393232 | tf_op jit(solution)/shard_map/reduce_scatter | solution.py:177
  334.1 2.0 broadcast_in_dim.27
  336.1 5.6 %all-to-all-start.3 = ((bf16[8,48,4096]{2,1,0:T(8,128)(2,1)}), bf16[8,48,4096]{2,1,0:T(8,128)(2,1)S(1)}, u32[]{:S(2)}, u32[]{:S(2)}) async-start(bf16[8,48,4096]{2,1,0:T(8,128)(2,1)} %broadcast_in_dim.27), calls=%async_computation.4 | async-start | bytes 6291456 | tf_op jit(solution)/shard_map/all_to_all | solution.py:22
  341.7 30.2 %all-reduce.4 = (f32[4096]{0:T(1024)S(1)}, f32[128]{0:T(128)S(1)}, f32[128]{0:T(128)S(1)}) all-reduce(f32[4096]{0:T(1024)S(1)} %get-tuple-element.36, f32[128]{0:T(128)S(1)} %get-tuple-element.38, f32[128]{0:T(128)S(1)} %get-tuple-element.40), channel_id=1, replica_groups=mesh['dp_0'=8,'dp_1'=2,'dp_2'=2,'tensor_0'=4,'tensor_1'=2] {'dp_0'}, use_global_device_ids=true, to_apply=%region_12.13 | all-reduce | flops 4352 | bytes 34816 | tf_op jit(solution)/shard_map/psum | solution.py:43
  371.9 11.1 %all-reduce.8 = (f32[4096]{0:T(1024)S(1)}, f32[128]{0:T(128)S(1)}, f32[128]{0:T(128)S(1)}) all-reduce(f32[4096]{0:T(1024)S(1)} %get-tuple-element.42, f32[128]{0:T(128)S(1)} %get-tuple-element.43, f32[128]{0:T(128)S(1)} %get-tuple-element.44), channel_id=1, replica_groups=mesh['dp_0'=8,'dp_1'=2,'dp_2'=2,'tensor_0'=4,'tensor_1'=2] {'dp_1'}, use_global_device_ids=true, to_apply=%region_13.14 | all-reduce | flops 4352 | bytes 34816 | tf_op jit(solution)/shard_map/psum | solution.py:43
  383.0 3.4 all-reduce.7
  386.3 15.4 %all-reduce.5 = (f32[4096]{0:T(1024)S(1)}, f32[128]{0:T(128)S(1)}, f32[128]{0:T(128)S(1)}) all-reduce(f32[4096]{0:T(1024)S(1)} %get-tuple-element.51, f32[128]{0:T(128)S(1)} %get-tuple-element.52, f32[128]{0:T(128)S(1)} %get-tuple-element.53), channel_id=1, replica_groups=mesh['dp_0'=8,'dp_1'=2,'dp_2'=2,'tensor_0'=4,'tensor_1'=2] {'tensor_0'}, use_global_device_ids=true, to_apply=%region_15.16 | all-reduce | flops 4352 | bytes 34816 | tf_op jit(solution)/shard_map/psum | solution.py:43
  401.8 8.0 %all-reduce.6 = (f32[4096]{0:T(1024)S(1)}, f32[128]{0:T(128)S(1)}, f32[128]{0:T(128)S(1)}) all-reduce(f32[4096]{0:T(1024)S(1)} %get-tuple-element.45, f32[128]{0:T(128)S(1)} %get-tuple-element.46, f32[128]{0:T(128)S(1)} %get-tuple-element.47), channel_id=1, replica_groups=mesh['dp_0'=8,'dp_1'=2,'dp_2'=2,'tensor_0'=4,'tensor_1'=2] {'tensor_1'}, use_global_device_ids=true, to_apply=%region_16.17 | all-reduce | flops 4352 | bytes 34816 | tf_op jit(solution)/shard_map/psum | solution.py:43
  410.9 89.4 %reduce-scatter.7.cloned.1.call-done = bf16[128,1280]{1,0:T(8,128)(2,1)} async-done(((bf16[4096,1280]{1,0:T(8,128)(2,1)}), bf16[128,1280]{1,0:T(8,128)(2,1)}) %reduce-scatter.7.cloned.1.call-update) | async-done | bytes 327696
  (115 shorter events, 37.2 us)
Async XLA Ops:
  72.2 8.3 %copy-start.10 = (bf16[128,768]{1,0:T(8,128)(2,1)S(1)}, bf16[128,768]{1,0:T(8,128)(2,1)}, u32[]{:S(2)}) copy-start(bf16[128,768]{1,0:T(8,128)(2,1)} %param.9) | copy-start | bytes 589828
  83.9 5.9 %copy-start = (bf16[384,4096]{1,0:T(8,128)(2,1)S(1)}, bf16[384,4096]{1,0:T(8,128)(2,1)}, u32[]{:S(2)}) copy-start(bf16[384,4096]{1,0:T(8,128)(2,1)} %param.7) | copy-start | bytes 9437188
  83.9 146.8 %all-to-all-start = ((bf16[32,128,768]{2,1,0:T(8,128)(2,1)}), bf16[32,128,768]{2,1,0:T(8,128)(2,1)}, u32[]{:S(2)}, u32[]{:S(2)}) async-start(bf16[32,128,768]{2,1,0:T(8,128)(2,1)} %stack.2), calls=%async_computation | async-start | bytes 12582912 | tf_op jit(solution)/shard_map/all_to_all | solution.py:131
  89.1 242.1 %reduce-scatter.5.cloned.1.call-start = ((), (), s32[]{:S(2)}) async-start(), calls=%async_computation.6 | async-start | bytes 3538944 | tf_op jit(solution)/shard_map/reduce_scatter | solution.py:177
  91.9 148.6 %copy-start.3 = (f32[384,64]{1,0:T(8,128)}, f32[384,64]{1,0:T(8,128)S(1)}, u32[]{:S(2)}) copy-start(f32[384,64]{1,0:T(8,128)S(1)} %get-tuple-element.66) | copy-start | bytes 294916
  91.9 3.2 copy-start.14
  95.1 135.6 %copy-start.11 = (f32[4096]{0:T(1024)S(1)}, f32[4096]{0:T(1024)}, u32[]{:S(2)}) copy-start(f32[4096]{0:T(1024)} %param.11) | copy-start | bytes 49156
  236.2 3.1 copy-start.27
  237.2 2.9 copy-start.22
  237.4 3.1 copy-start.18
  238.2 2.6 copy-start.12
  238.3 2.6 copy-start.16
  241.8 3.8 copy-start.20
  248.6 2.7 copy-start.28
  248.6 3.5 copy-start.17
  248.6 3.5 copy-start.25
  248.6 4.7 copy-start.19
  248.7 6.0 %copy-start.30 = (bf16[384,128]{0,1:T(8,128)(2,1)S(1)}, bf16[384,128]{0,1:T(8,128)(2,1)}, u32[]{:S(2)}) copy-start(bf16[384,128]{0,1:T(8,128)(2,1)} %fusion.20) | copy-start | bytes 294916
  251.3 3.3 copy-start.8
  261.8 238.5 %reduce-scatter.7.cloned.1.call-start = ((), (), s32[]{:S(2)}) async-start(), calls=%async_computation.7 | async-start | bytes 10813440
  264.7 2.4 copy-start.1
  264.7 2.4 copy-start.9
  264.7 2.4 copy-start.29
  336.1 74.8 %all-to-all-start.3 = ((bf16[8,48,4096]{2,1,0:T(8,128)(2,1)}), bf16[8,48,4096]{2,1,0:T(8,128)(2,1)S(1)}, u32[]{:S(2)}, u32[]{:S(2)}) async-start(bf16[8,48,4096]{2,1,0:T(8,128)(2,1)} %broadcast_in_dim.27), calls=%async_computation.4 | async-start | bytes 6291456 | tf_op jit(solution)/shard_map/all_to_all | solution.py:22
  (11 other events, 15.1 us)
Sparse Core Ops, SparseCore 0:
  261.9 69.2 reduce-scatter.4
  335.7 164.5 reduce-scatter.6
